TPU v7x, 32 devices: a whole 2x2x4 slice. The times are simulated.
32 devices in a mesh: seq: 8 (over z, x), head: 4 (over y, core).
Axes of the slice: x: 2, y: 2, z: 4, core: 2. Of those that a mesh axis runs over, the one named last changes fastest.
Arguments:
- query_in: bfloat16 [2048, 8192], P('seq', 'head'), may hold values from -1.796875 to 1.796875
- key_in: bfloat16 [2048, 8192], P('seq', 'head'), may hold values from -1.796875 to 1.796875
- value_in: bfloat16 [2048, 8192], P('seq', 'head'), may hold values from -11 to 11
- log_decay: float32 [2048, 64], P('seq', 'head'), may hold values from -1 to 0, as said below
- norm_gain: float32 [8192], P('head'), may hold values from 0.5 to 1.5
- prompt_lengths: int32 [4], replicated, may hold values from 1 to 1536, 2048 in all
- step_query: bfloat16 [4, 128, 8192], P(None, 'seq', 'head'), may hold values from -1.796875 to 1.796875
- step_key: bfloat16 [4, 128, 8192], P(None, 'seq', 'head'), may hold values from -1.796875 to 1.796875
- step_value: bfloat16 [4, 128, 8192], P(None, 'seq', 'head'), may hold values from -6 to 6
- step_decay: float32 [4, 128, 64], P(None, 'seq', 'head'), may hold values from -0.3 to -0.01
- row_prompt: int32 [128], P('seq'), may hold values from 0 to 3
Outputs:
- attn_out: bfloat16 [2048, 8192], P('seq', 'head')
- decode_out: bfloat16 [4, 128, 8192], P(None, 'seq', 'head')
Inputs may be any that keep to these rules, and one draw needn't show every extreme that they name: `log_decay`: Negative; per head and token.
All inputs are finite; a program needn't handle non-finite values.
Results may differ from a plain program's by a relative error of at most 0.0056.
Values sent between devices are 32-bit elements; how exact they have to be, the bound alone decides.
A program may use at most 64 MiB of HBM per device.

v0:
```python
import jax
import jax.numpy as jnp
from jax import lax
from jax.sharding import PartitionSpec as P

HEAD_COUNT = 64
HDIM = 128
BLOCK = 256
PROMPTS = 4
EPSILON = 1e-06


def carried_in(part, axis, combine, identity):
    place = lax.axis_index(axis)
    gathered = jax.tree.map(lambda a: lax.all_gather(a, axis), part)
    state = jax.tree.map(lambda a, e: jnp.zeros_like(a) + jnp.asarray(e, a.dtype), part, identity)

    def one(step, state):
        return combine(
            state, jax.tree.map(lambda a: lax.dynamic_index_in_dim(a, step, 0, False), gathered)
        )

    return lax.fori_loop(0, place, one, state)


def segment_ids(prompt_lengths, positions):
    boundary = jnp.cumsum(prompt_lengths)
    return jnp.sum((positions[:, None] >= boundary[None, :]).astype(jnp.int32), axis=1)


def combine_pairs(earlier, later):
    return (earlier[0] * later[0], later[0][:, None, None] * earlier[1] + later[1])


def local(
    query_in,
    key_in,
    value_in,
    log_decay,
    norm_gain,
    prompt_lengths,
    step_query,
    step_key,
    step_value,
    step_decay,
    row_prompt,
):
    tok_count = query_in.shape[0]
    heads_here = log_decay.shape[1]
    nblocks = tok_count // BLOCK
    first = lax.axis_index("seq") * tok_count
    positions = first + jnp.arange(tok_count, dtype=jnp.int32)
    segs = segment_ids(prompt_lengths, positions)
    seg_entry = jnp.where(first > 0, segment_ids(prompt_lengths, (first - 1)[None])[0], -1)
    shape4 = (nblocks, BLOCK, heads_here, HDIM)
    queries = query_in.reshape(shape4)
    keys_blk = key_in.reshape(shape4)
    values_blk = value_in.reshape(shape4)
    cumul = jnp.cumsum(log_decay.reshape(nblocks, BLOCK, heads_here), axis=1)
    seg_blocks = segs.reshape(nblocks, BLOCK)
    seg_front = jnp.concatenate([seg_entry[None], seg_blocks[:-1, -1]])
    causal = jnp.arange(BLOCK)[:, None] >= jnp.arange(BLOCK)[None, :]
    linked = (causal[None] & (seg_blocks[:, :, None] == seg_blocks[:, None, :]))[:, None]
    cum_heads = jnp.transpose(cumul, (0, 2, 1))
    spread = cum_heads[:, :, :, None] - cum_heads[:, :, None, :]
    factor = jnp.where(linked, jnp.exp(jnp.where(linked, spread, 0.0)), 0.0)
    scores = jnp.einsum("nthd,nshd->nhts", queries, keys_blk, preferred_element_type=jnp.float32)
    weights = (scores * factor).astype(jnp.bfloat16)
    inner = jnp.einsum("nhts,nshd->nthd", weights, values_blk, preferred_element_type=jnp.float32)
    keep = (
        jnp.exp(cumul[:, -1:, :] - cumul)
        * (seg_blocks == seg_blocks[:, -1:]).astype(jnp.float32)[:, :, None]
    )
    keyed = (keys_blk.astype(jnp.float32) * keep[..., None]).astype(jnp.bfloat16)
    updates = jnp.einsum("nshd,nshe->nhde", keyed, values_blk, preferred_element_type=jnp.float32)
    onward = (
        jnp.exp(cumul[:, -1, :]) * (seg_blocks[:, -1] == seg_front).astype(jnp.float32)[:, None]
    )
    local_states = [jnp.zeros((heads_here, HDIM, HDIM), jnp.float32)]
    growth = [jnp.ones((heads_here,), jnp.float32)]
    blk_index = 0
    local_states.append(onward[blk_index][:, None, None] * local_states[-1] + updates[blk_index])
    growth.append(onward[blk_index] * growth[-1])
    summary = (growth[-1], local_states[-1])
    identity = (
        jnp.ones((heads_here,), jnp.float32),
        jnp.zeros((heads_here, HDIM, HDIM), jnp.float32),
    )
    entry = carried_in(summary, "seq", combine_pairs, identity)
    entry_state = entry[1]
    start_states = jnp.stack([local_states[0] + growth[0][:, None, None] * entry_state])
    state_half = start_states.astype(jnp.bfloat16)
    carried = jnp.exp(cumul) * (seg_blocks == seg_front[:, None]).astype(jnp.float32)[:, :, None]
    outer = (
        jnp.einsum("nthd,nhde->nthe", queries, state_half, preferred_element_type=jnp.float32)
        * carried[..., None]
    )
    mixed = (inner + outer).reshape(tok_count, heads_here * HDIM)
    squares = lax.psum(jnp.sum(mixed * mixed, axis=1), "head")
    scale = lax.rsqrt(squares / (HEAD_COUNT * HDIM) + EPSILON)
    attn_out = (mixed * scale[:, None] * norm_gain[None, :]).astype(jnp.bfloat16)
    boundary = jnp.cumsum(prompt_lengths)

    def prompt_end(prompt):
        last_tok = boundary[prompt] - 1
        local_tok = last_tok - first
        owned = (local_tok >= 0) & (local_tok < tok_count)
        safe_tok = jnp.clip(local_tok, 0, tok_count - 1)
        blk_index = safe_tok // BLOCK
        offset = safe_tok - blk_index * BLOCK
        cum_blk = cumul[blk_index]
        reached = cum_blk[offset]
        taken = (jnp.arange(BLOCK) <= offset) & (seg_blocks[blk_index] == prompt)
        keep_end = (
            jnp.exp(jnp.where(taken[:, None], reached[None, :] - cum_blk, 0.0))
            * taken.astype(jnp.float32)[:, None]
        )
        tailed = (keys_blk[blk_index].astype(jnp.float32) * keep_end[:, :, None]).astype(
            jnp.bfloat16
        )
        part = jnp.einsum(
            "shd,she->hde", tailed, values_blk[blk_index], preferred_element_type=jnp.float32
        )
        lead = jnp.exp(reached) * (seg_front[blk_index] == prompt).astype(jnp.float32)
        total = lead[:, None, None] * start_states[blk_index] + part
        return total * owned.astype(jnp.float32)

    candidates = lax.map(prompt_end, jnp.arange(PROMPTS, dtype=jnp.int32))
    prompt_state = lax.psum(candidates, "seq")
    rows_here = row_prompt.shape[0]
    row_states = jnp.take(prompt_state, row_prompt, axis=0)
    results = []
    for section in range(step_query.shape[0]):
        query_now = step_query[section].astype(jnp.float32).reshape(rows_here, heads_here, HDIM)
        key_now = step_key[section].astype(jnp.float32).reshape(rows_here, heads_here, HDIM)
        value_now = step_value[section].astype(jnp.float32).reshape(rows_here, heads_here, HDIM)
        row_states = (
            jnp.exp(step_decay[section])[:, :, None, None] * row_states
            + key_now[:, :, :, None] * value_now[:, :, None, :]
        )
        results.append(
            jnp.einsum(
                "rhd,rhde->rhe", query_now, row_states, precision=lax.Precision.HIGHEST
            ).reshape(rows_here, heads_here * HDIM)
        )
    decoded = jnp.stack(results)
    step_squares = lax.psum(jnp.sum(decoded * decoded, axis=2), "head")
    step_scale = lax.rsqrt(step_squares / (HEAD_COUNT * HDIM) + EPSILON)
    decode_out = (decoded * step_scale[:, :, None] * norm_gain[None, None, :]).astype(jnp.bfloat16)
    return (attn_out, decode_out)


def solution(mesh):
    in_specs = (
        P("seq", "head"),
        P("seq", "head"),
        P("seq", "head"),
        P("seq", "head"),
        P("head"),
        P(),
        P(None, "seq", "head"),
        P(None, "seq", "head"),
        P(None, "seq", "head"),
        P(None, "seq", "head"),
        P("seq"),
    )
    out_specs = (P("seq", "head"), P(None, "seq", "head"))
    return jax.shard_map(local, mesh=mesh, in_specs=in_specs, out_specs=out_specs, check_vma=False)
```

profile of v0, /device:TPU:0, one launch (start us, length us, event | category | flops | bytes accessed | tf_op | source)
XLA Modules:
  0.0 465.3 jit_solution(464305001508278530)
XLA Ops:
  7.2 0.8 copy_bitcast_fusion
  8.8 0.8 reduce-window.10
  9.6 0.7 fusion.50
  10.4 0.6 slice.86
  11.7 0.7 compare_convert_fusion.1
  13.3 1.5 copy.146
  14.8 2.6 convolution_add_fusion.1
  17.6 1.5 copy.133
  19.1 1.4 copy.135
  20.5 22.7 %all-gather = f32[8,1,16]{2,1,0:T(1,128)S(1)} all-gather(f32[1,1,16]{2,1,0:T(1,128)S(1)} %get-tuple-element.344), channel_id=2, replica_groups=mesh['seq'=8,'head'=4] {'seq'}, dimensions={0}, use_global_device_ids=true | all-gather | bytes 576 | tf_op jit(solution)/shard_map/all_gather | solution.py:15
  43.2 101.7 %all-gather.4.cloned.1.call-done = f32[128,128,128]{2,1,0:T(8,128)} async-done(((f32[16,128,128]{2,1,0:T(8,128)}), f32[128,128,128]{2,1,0:T(8,128)}) %all-gather.4.cloned.1.call-update) | async-done | bytes 8388624 | tf_op jit(solution)/shard_map/all_gather | solution.py:15
  145.0 32.4 %while.26 = (s32[]{:T(128)}, f32[4,16,128,128]{3,2,1,0:T(8,128)}, s32[4]{0:T(128)S(1)}, s32[4]{0:T(128)S(1)}, s32[]{:T(128)}, /*index=5*/f32[1,256,16]{1,2,0:T(8...) while((s32[]{:T(128)}, f32[4,16,128,128]{3,2,1,0:T(8,128)}, ...), condition=%wide.region_10.11_spmd, body=%wide.region_9.10_spmd.sunk | while | flops 136590384 | bytes 4248923 | solution.py:128
  145.0 0.6 dynamic_slice.45
  147.6 0.6 dynamic_slice.46
  149.0 0.7 compare_reduce_fusion.2
  150.4 2.7 fusion.78
  153.2 0.6 dynamic_slice.45
  155.7 0.6 dynamic_slice.46
  157.2 0.7 compare_reduce_fusion.2
  158.6 2.6 fusion.78
  163.8 0.6 dynamic_slice.46
  165.2 0.7 compare_reduce_fusion.2
  166.7 2.7 fusion.78
  171.9 0.6 dynamic_slice.46
  173.3 0.7 compare_reduce_fusion.2
  174.7 2.6 fusion.78
  177.4 1.6 convert_bitcast_fusion.1
  179.1 0.7 copy.151
  179.7 1.7 convert_bitcast_fusion
  181.4 0.7 copy.152
  182.1 0.7 copy.153
  182.7 0.7 copy.154
  183.4 1.6 fusion.54
  185.0 1.6 reshape.536
  186.6 1.6 reshape.534
  188.2 1.6 copy.155
  189.8 1.6 copy.156
  191.4 1.6 reshape.538
  193.0 0.7 copy.157
  193.7 1.6 copy.158
  195.2 0.8 reshape.540
  196.2 0.6 compare_and_fusion.1
  196.8 1.4 exponential_bitcast_fusion
  198.2 4.4 fusion.36
  202.6 4.1 multiply_reduce_fusion
  206.7 1.9 copy.131
  208.7 133.8 %all-reduce.3.cloned.1.call-done = f32[4,16,128,128]{3,2,1,0:T(8,128)} async-done(((f32[4,16,128,128]{3,2,1,0:T(8,128)}), f32[4,16,128,128]{3,2,1,0:T(8,128)}) %all-reduce.3.cloned.1.call-update) | async-done | bytes 4194320 | tf_op jit(solution)/shard_map/psum | solution.py:129
  342.5 10.0 %gather_fusion = f32[16,16,128,128]{3,2,1,0:T(8,128)} fusion(f32[4,16,128,128]{3,2,1,0:T(8,128)} %all-reduce.3.cloned.1.call-done, s32[1024]{0:T(1024)S(1)} %pad_clamp_fusion), kind=kCustom, calls=%fused_computation | custom fusion | bytes 33554496 | tf_op jit(solution)/shard_map/jit(_take)/gather | solution.py:131
  352.5 17.9 %fusion.15 = f32[16,16,1,128]{3,2,1,0:T(1,128)} fusion(bf16[16,16,128,1]{2,3,1,0:T(2,128)(2,1)S(1)} %copy-done.3, f32[16,16,128]{2,1,0:T(8,128)} %bitcast.215, f32[16,16,128]{2,1,0:T(8,128)} %bitcast.212, f32[16,16]{1,0:T(8,128)S(1)} %get-tuple-element.346, f32[16,16,128,128]{3,2,1,0:T(8,128)} %gather_fusion, f32[16,16,128]{2,1,0:T(8,128)} %bitcast.208, ...), kind=kOutput, calls=%fused_computation.28 | convolution fusion | flops 79691776 | bytes 17500176 | tf_op jit(solution)/shard_map/rhd,rhde->rhe/dot_general | solution.py:142
  370.4 0.9 stack_reshape.13
  371.4 13.4 %fusion.52 = f32[16,16,1,128]{3,2,1,0:T(1,128)} fusion(bf16[16,16,128,1]{2,3,1,0:T(2,128)(2,1)S(1)} %copy-done.2, f32[16,16,128,128]{3,2,1,0:T(8,128)} %gather_fusion, f32[16,16,128]{2,1,0:T(8,128)} %bitcast.209, f32[16,16,128]{2,1,0:T(8,128)S(1)} %bitcast.207, f32[16,16]{1,0:T(8,128)} %get-tuple-element.347, pred[16]{0:T(512)(128)(4,1)} %compare_and_fusion.1), kind=kOutput, calls=%fused_computation.108 | convolution fusion | flops 67108864 | bytes 17237008 | tf_op jit(solution)/shard_map/rhd,rhde->rhe/dot_general | solution.py:142
  384.8 0.9 stack_reshape.12
  385.7 0.7 constant_dynamic-update-slice_fusion.3
  386.4 22.6 %fusion.16 = f32[16,16,1,128]{3,2,1,0:T(1,128)} fusion(bf16[16,16,128,1]{2,3,1,0:T(2,128)(2,1)} %reshape.538, f32[16,16,128]{2,1,0:T(8,128)} %bitcast.220, f32[16,16,128]{2,1,0:T(8,128)} %bitcast.218, f32[16,16]{1,0:T(8,128)} %get-tuple-element.348, f32[16,16,128]{2,1,0:T(8,128)} %bitcast.216, f32[16,16,128]{2,1,0:T(8,128)} %bitcast.213, ...), kind=kOutput, calls=%fused_computation.29 | convolution fusion | flops 92274688 | bytes 17763344 | tf_op jit(solution)/shard_map/rhd,rhde->rhe/dot_general | solution.py:142
  409.0 0.9 stack_reshape.14
  409.9 34.9 %fusion.11 = f32[16,16,1,128]{3,2,1,0:T(1,128)} fusion(bf16[16,16,128,1]{2,3,1,0:T(2,128)(2,1)S(1)} %copy-done.1, f32[16,16,128]{2,1,0:T(8,128)} %bitcast.223, f32[16,16,128]{2,1,0:T(8,128)} %bitcast.222, f32[16,16]{1,0:T(8,128)S(1)} %get-tuple-element.345, f32[16,16,128]{2,1,0:T(8,128)} %bitcast.221, f32[16,16,128]{2,1,0:T(8,128)} %bitcast.219, ...), kind=kOutput, calls=%fused_computation.21 | convolution fusion | flops 104857600 | bytes 18026512 | tf_op jit(solution)/shard_map/rhd,rhde->rhe/dot_general | solution.py:142
  444.8 0.9 stack_reshape.15
  445.8 0.7 constant_dynamic-update-slice_fusion.2
  446.5 0.7 constant_dynamic-update-slice_fusion.1
  447.1 0.7 constant_dynamic-update-slice_fusion
  447.8 1.2 multiply_reduce_fusion.1
  448.9 6.4 %all-reduce = (f32[256]{0:T(256)S(1)}, f32[4,16]{1,0:T(4,128)S(1)}) all-reduce(f32[256]{0:T(256)} %get-tuple-element.351, f32[4,16]{1,0:T(4,128)S(1)} %multiply_reduce_fusion.1), channel_id=1, replica_groups=mesh['seq'=8,'head'=4] {'head'}, use_global_device_ids=true, to_apply=%region_8.9 | all-reduce | flops 320 | bytes 2560 | tf_op jit(solution)/shard_map/psum | solution.py:99
  455.4 1.9 multiply_convert_fusion.4
  457.2 1.2 multiply_convert_fusion.1
  (66 shorter events, 4.1 us)
Async XLA Ops:
  7.2 191.1 %copy-start = (bf16[256,2048]{1,0:T(8,128)(2,1)S(1)}, bf16[256,2048]{1,0:T(8,128)(2,1)}, u32[]{:S(2)}) copy-start(bf16[256,2048]{1,0:T(8,128)(2,1)} %param.15) | copy-start | bytes 3145732
  7.2 137.7 %all-gather.4.cloned.1.call-start = ((), (), s32[]{:S(2)}) async-start(), calls=%async_computation.1 | async-start | bytes 9437184 | tf_op jit(solution)/shard_map/all_gather | solution.py:15
  17.5 325.0 %all-reduce.3.cloned.1.call-start = ((), (), s32[]{:S(2)}) async-start(), calls=%async_computation | async-start | bytes 8388608 | tf_op jit(solution)/shard_map/psum | solution.py:129
  145.0 51.2 %copy-start.7 = (s32[16]{0:T(128)S(1)}, s32[16]{0:T(128)}, u32[]{:S(2)}) copy-start(s32[16]{0:T(128)} %param.25) | copy-start | bytes 196
  198.1 188.2 %copy-start.6 = (f32[16,16]{1,0:T(8,128)}, f32[16,16]{1,0:T(8,128)S(1)}, u32[]{:S(2)}) copy-start(f32[16,16]{1,0:T(8,128)S(1)} %get-tuple-element.346) | copy-start | bytes 3076
  208.6 143.9 %copy-start.3 = (bf16[16,16,128,1]{2,3,1,0:T(2,128)(2,1)S(1)}, bf16[16,16,128,1]{2,3,1,0:T(2,128)(2,1)}, u32[]{:S(2)}) copy-start(bf16[16,16,128,1]{2,3,1,0:T(2,128)(2,1)} %reshape.536) | copy-start | bytes 196612
  208.7 143.8 %copy-start.4 = (f32[2,8,16,128]{3,2,1,0:T(8,128)S(1)}, f32[2,8,16,128]{3,2,1,0:T(8,128)}, u32[]{:S(2)}) copy-start(f32[2,8,16,128]{3,2,1,0:T(8,128)} %copy.151) | copy-start | bytes 393220
  352.5 18.9 %copy-start.2 = (bf16[16,16,128,1]{2,3,1,0:T(2,128)(2,1)S(1)}, bf16[16,16,128,1]{2,3,1,0:T(2,128)(2,1)}, u32[]{:S(2)}) copy-start(bf16[16,16,128,1]{2,3,1,0:T(2,128)(2,1)} %reshape.534) | copy-start | bytes 196612
  386.4 23.6 %copy-start.1 = (bf16[16,16,128,1]{2,3,1,0:T(2,128)(2,1)S(1)}, bf16[16,16,128,1]{2,3,1,0:T(2,128)(2,1)}, u32[]{:S(2)}) copy-start(bf16[16,16,128,1]{2,3,1,0:T(2,128)(2,1)} %reshape.540) | copy-start | bytes 196612
  409.9 45.4 %copy-start.5 = (f32[2048]{0:T(1024)S(1)}, f32[2048]{0:T(1024)}, u32[]{:S(2)}) copy-start(f32[2048]{0:T(1024)} %param.19) | copy-start | bytes 24580
Sparse Core Ops, SparseCore 0:
  17.6 127.2 all-gather.3
  177.5 164.8 all-reduce.2
where the time goes:
time: 467 us; the launch traced here: 465 us
  waiting for transfers between devices  235 us (50%)
  matrix products  111 us (24%)
  local copies, waits for them, and re-layouts  46.8 us (10%)
  blocking collectives  29.1 us (6%)
  between operations  15.6 us (3%)
  other arithmetic  14.4 us (3%)
  loops' own time  13.2 us (3%)
    psum x1, waiting for transfers between devices, local(): prompt_state = lax.psum(candidates, 'seq')  134 us
    all_gather x1, waiting for transfers between devices, carried_in(): gathered = jax.tree.map(lambda a: lax.all_gather(a, axis), part)  102 us
    dot_general x4, matrix products, local(): jnp.einsum('rhd,rhde->rhe', query_now, row_states, precision=lax.Precisio...  88.8 us
    all_gather x1, blocking collectives, carried_in(): gathered = jax.tree.map(lambda a: lax.all_gather(a, axis), part)  22.7 us
    another operation x1, loops' own time, local(): candidates = lax.map(prompt_end, jnp.arange(PROMPTS, dtype=jnp.int32))  13.2 us
    unnamed x28, local copies, waits for them, and re-layouts  11.6 us
    dot_general x4, matrix products, prompt_end(): jnp.einsum('shd,she->hde', tailed, values_blk[blk_index], preferred_eleme...  10.7 us
    gather x1, local copies, waits for them, and re-layouts, local(): row_states = jnp.take(prompt_state, row_prompt, axis=0)  10 us
  transfers between devices with their start and end apart: 2, of which 2 were waited for; matrix products, arithmetic and copies ran while one was open for 7% of the time, Pallas kernels for 0%

commit v1 on v0

--- a/solution.py
+++ b/solution.py
@@ -126,7 +126,10 @@
         return total * owned.astype(jnp.float32)
 
     candidates = lax.map(prompt_end, jnp.arange(PROMPTS, dtype=jnp.int32))
-    prompt_state = lax.psum(candidates, "seq")
+    devices, prompt_state = (lax.axis_size("seq"), candidates)
+    for hop in [1 << k for k in range(devices.bit_length() - 1)]:
+        pairs = [(i, i ^ hop) for i in range(devices)]
+        prompt_state = prompt_state + lax.ppermute(prompt_state, "seq", pairs)
     rows_here = row_prompt.shape[0]
     row_states = jnp.take(prompt_state, row_prompt, axis=0)
     results = []

time: 467 us -> 682 us (1.46)
  waiting for transfers between devices: 235 us -> 439 us
  starting transfers between devices: 0.08 us -> 14.5 us
  other arithmetic: 14.4 us -> 22.2 us
  local copies, waits for them, and re-layouts: 46.8 us -> 39.5 us
    ppermute x0 -> x3, waiting for transfers between devices: none -> 337 us  [local(): prompt_state = prompt_state + lax.ppermute(prompt_state, 'seq', pairs)]
    psum x1 -> x0, waiting for transfers between devices: 134 us -> none  [local(): prompt_state = lax.psum(candidates, 'seq')]
    ppermute x0 -> x3, starting transfers between devices: none -> 14.5 us  [local(): prompt_state = prompt_state + lax.ppermute(prompt_state, 'seq', pairs)]
    add x0 -> x3, other arithmetic: none -> 12.1 us  [local(): prompt_state = prompt_state + lax.ppermute(prompt_state, 'seq', pairs)]
  transfers between devices with their start and end apart: 2 -> 4, of which waited for: 2 -> 4; matrix products, arithmetic and copies ran while one was open for 7% -> 4% of each run, Pallas kernels for 0% -> 0%
where the time goes in v1:
time: 682 us; the launch traced here: 681 us
  waiting for transfers between devices  439 us (64%)
  matrix products  109 us (16%)
  local copies, waits for them, and re-layouts  39.5 us (6%)
  blocking collectives  28.6 us (4%)
  other arithmetic  22.2 us (3%)
  between operations  15.7 us (2%)
  starting transfers between devices  14.5 us (2%)
  loops' own time  13.2 us (2%)
    ppermute x3, waiting for transfers between devices, local(): prompt_state = prompt_state + lax.ppermute(prompt_state, 'seq', pairs)  337 us
    all_gather x1, waiting for transfers between devices, carried_in(): gathered = jax.tree.map(lambda a: lax.all_gather(a, axis), part)  102 us
    dot_general x4, matrix products, local(): jnp.einsum('rhd,rhde->rhe', query_now, row_states, precision=lax.Precisio...  87 us
    all_gather x1, blocking collectives, carried_in(): gathered = jax.tree.map(lambda a: lax.all_gather(a, axis), part)  22.7 us
    ppermute x3, starting transfers between devices, local(): prompt_state = prompt_state + lax.ppermute(prompt_state, 'seq', pairs)  14.5 us
  transfers between devices with their start and end apart: 4, of which 4 were waited for; matrix products, arithmetic and copies ran while one was open for 4% of the time, Pallas kernels for 0%

profile of v1, /device:TPU:0, one launch (start us, length us, event | category | flops | bytes accessed | tf_op | source)
XLA Modules:
  0.0 680.9 jit_solution(9765093756036271642)
XLA Ops:
  7.2 0.8 copy_bitcast_fusion
  8.8 0.8 reduce-window.10
  9.6 0.7 fusion.50
  10.4 0.6 slice.86
  11.7 0.7 compare_convert_fusion.1
  13.3 1.5 copy.146
  14.8 2.6 convolution_add_fusion.1
  17.6 1.5 copy.133
  19.1 1.3 copy.135
  20.4 22.7 %all-gather = f32[8,1,16]{2,1,0:T(1,128)S(1)} all-gather(f32[1,1,16]{2,1,0:T(1,128)S(1)} %get-tuple-element.344), channel_id=2, replica_groups=mesh['seq'=8,'head'=4] {'seq'}, dimensions={0}, use_global_device_ids=true | all-gather | bytes 576 | tf_op jit(solution)/shard_map/all_gather | solution.py:15
  43.1 101.7 %all-gather.4.cloned.1.call-done = f32[128,128,128]{2,1,0:T(8,128)} async-done(((f32[16,128,128]{2,1,0:T(8,128)}), f32[128,128,128]{2,1,0:T(8,128)}) %all-gather.4.cloned.1.call-update) | async-done | bytes 8388624 | tf_op jit(solution)/shard_map/all_gather | solution.py:15
  145.0 32.3 %while.26 = (s32[]{:T(128)}, f32[4,16,128,128]{3,2,1,0:T(8,128)}, s32[4]{0:T(128)S(1)}, s32[4]{0:T(128)S(1)}, s32[]{:T(128)}, /*index=5*/f32[1,256,16]{1,2,0:T(8...) while((s32[]{:T(128)}, f32[4,16,128,128]{3,2,1,0:T(8,128)}, ...), condition=%wide.region_10.11_spmd, body=%wide.region_9.10_spmd.sunk | while | flops 136590384 | bytes 4248923 | solution.py:128
  145.0 0.6 dynamic_slice.45
  147.5 0.6 dynamic_slice.46
  149.0 0.7 compare_reduce_fusion.2
  150.4 2.7 fusion.78
  155.7 0.6 dynamic_slice.46
  157.1 0.7 compare_reduce_fusion.2
  158.6 2.6 fusion.78
  163.7 0.6 dynamic_slice.46
  165.2 0.7 compare_reduce_fusion.2
  166.6 2.7 fusion.78
  169.3 0.6 dynamic_slice.45
  171.8 0.6 dynamic_slice.46
  173.2 0.7 compare_reduce_fusion.2
  174.7 2.7 fusion.78
  177.4 2.1 collective-permute-start
  179.5 90.1 %collective-permute-done = f32[4,16,128,128]{3,2,1,0:T(8,128)S(1)} collective-permute-done((f32[4,16,128,128]{3,2,1,0:T(8,128)}, f32[4,16,128,128]{3,2,1,0:T(8,128)S(1)}, u32[]{:S(2)}, u32[]{:S(2)}) %collective-permute-start) | collective-permute-done | bytes 4194336 | tf_op jit(solution)/shard_map/ppermute | solution.py:132
  269.5 2.9 add.130
  272.5 2.9 collective-permute-start.1
  275.4 89.5 %collective-permute-done.1 = f32[4,16,128,128]{3,2,1,0:T(8,128)S(1)} collective-permute-done((f32[4,16,128,128]{3,2,1,0:T(8,128)S(1)}, f32[4,16,128,128]{3,2,1,0:T(8,128)S(1)}, u32[]{:S(2)}, u32[]{:S(2)}) %collective-permute-start.1) | collective-permute-done | bytes 4194336 | tf_op jit(solution)/shard_map/ppermute | solution.py:132
  364.9 2.7 add.131
  367.6 9.5 %collective-permute-start.2 = (f32[4,16,128,128]{3,2,1,0:T(8,128)}, f32[4,16,128,128]{3,2,1,0:T(8,128)}, u32[]{:S(2)}, u32[]{:S(2)}) collective-permute-start(f32[4,16,128,128]{3,2,1,0:T(8,128)} %add.131), channel_id=1, source_target_pairs={{0,16},{4,20},{8,24},{12,28},{16,0},{20,4},{24,8},{28,12},{1,17},{... | collective-permute-start | bytes 12582920 | tf_op jit(solution)/shard_map/ppermute | solution.py:132
  377.1 0.7 copy.151
  377.8 0.7 copy.152
  378.5 0.7 copy.153
  379.2 0.7 copy.154
  379.9 0.7 copy.155
  380.6 0.7 copy.156
  381.3 0.7 copy.157
  381.9 0.7 copy.158
  382.6 0.6 fusion.54
  383.3 1.6 reshape.540
  384.9 0.7 reshape.538
  385.6 0.7 reshape.536
  386.3 0.7 reshape.534
  387.8 1.3 exponential_bitcast_fusion
  389.3 4.3 fusion.36
  393.6 4.0 multiply_reduce_fusion
  397.6 1.9 copy.131
  399.5 157.3 %collective-permute-done.2 = f32[4,16,128,128]{3,2,1,0:T(8,128)} collective-permute-done((f32[4,16,128,128]{3,2,1,0:T(8,128)}, f32[4,16,128,128]{3,2,1,0:T(8,128)}, u32[]{:S(2)}, u32[]{:S(2)}) %collective-permute-start.2) | collective-permute-done | bytes 4194336 | tf_op jit(solution)/shard_map/ppermute | solution.py:132
  556.8 6.5 add.132
  563.3 10.1 %gather_fusion = f32[16,16,128,128]{3,2,1,0:T(8,128)} fusion(f32[4,16,128,128]{3,2,1,0:T(8,128)} %add.132, s32[1024]{0:T(1024)S(1)} %pad_clamp_fusion), kind=kCustom, calls=%fused_computation | custom fusion | bytes 33554496 | tf_op jit(solution)/shard_map/jit(_take)/gather | solution.py:134
  573.6 32.5 %fusion.11 = f32[16,16,1,128]{3,2,1,0:T(1,128)S(1)} fusion(bf16[16,16,128,1]{2,3,1,0:T(2,128)(2,1)S(1)} %copy-done.8, f32[16,16,128]{2,1,0:T(8,128)S(1)} %bitcast.223, f32[16,16,128]{2,1,0:T(8,128)S(1)} %bitcast.222, f32[16,16]{1,0:T(8,128)} %get-tuple-element.345, f32[16,16,128]{2,1,0:T(8,128)S(1)} %bitcast.220, f32[16,16,128]{2,1,0:T(8,128)S(1)} %bitcast.218, ...), kind=kOutput, calls=%fused_computation.21 | convolution fusion | flops 104857600 | bytes 18026512 | tf_op jit(solution)/shard_map/rhd,rhde->rhe/dot_general | solution.py:145
  606.1 23.1 %fusion.16 = f32[16,16,1,128]{3,2,1,0:T(1,128)S(1)} fusion(bf16[16,16,128,1]{2,3,1,0:T(2,128)(2,1)S(1)} %copy-done.7, f32[16,16,128]{2,1,0:T(8,128)S(1)} %bitcast.221, f32[16,16,128]{2,1,0:T(8,128)S(1)} %bitcast.219, f32[16,16]{1,0:T(8,128)} %get-tuple-element.348, f32[16,16,128]{2,1,0:T(8,128)S(1)} %bitcast.217, f32[16,16,128]{2,1,0:T(8,128)S(1)} %bitcast.214, ...), kind=kOutput, calls=%fused_computation.29 | convolution fusion | flops 92274688 | bytes 17763344 | tf_op jit(solution)/shard_map/rhd,rhde->rhe/dot_general | solution.py:145
  629.2 18.0 %fusion.15 = f32[16,16,1,128]{3,2,1,0:T(1,128)} fusion(bf16[16,16,128,1]{2,3,1,0:T(2,128)(2,1)S(1)} %copy-done.6, f32[16,16,128]{2,1,0:T(8,128)} %bitcast.215, f32[16,16,128]{2,1,0:T(8,128)} %bitcast.212, f32[16,16]{1,0:T(8,128)S(1)} %get-tuple-element.346, f32[16,16,128,128]{3,2,1,0:T(8,128)} %gather_fusion, f32[16,16,128]{2,1,0:T(8,128)} %bitcast.208, ...), kind=kOutput, calls=%fused_computation.28 | convolution fusion | flops 79691776 | bytes 17500176 | tf_op jit(solution)/shard_map/rhd,rhde->rhe/dot_general | solution.py:145
  647.3 0.9 stack_reshape.13
  648.2 13.4 %fusion.52 = f32[16,16,1,128]{3,2,1,0:T(1,128)} fusion(bf16[16,16,128,1]{2,3,1,0:T(2,128)(2,1)} %reshape.534, f32[16,16,128,128]{3,2,1,0:T(8,128)} %gather_fusion, f32[16,16,128]{2,1,0:T(8,128)} %bitcast.209, f32[16,16,128]{2,1,0:T(8,128)} %bitcast.205, f32[16,16]{1,0:T(8,128)S(1)} %get-tuple-element.347, pred[16]{0:T(512)(128)(4,1)} %compare_and_fusion.1), kind=kOutput, calls=%fused_computation.108 | convolution fusion | flops 67108864 | bytes 17237008 | tf_op jit(solution)/shard_map/rhd,rhde->rhe/dot_general | solution.py:145
  661.6 1.6 stack_reshape.12
  663.2 0.9 constant_dynamic-update-slice_fusion.3
  664.2 0.8 copy-done.2
  665.1 5.8 all-reduce
  671.0 1.9 multiply_convert_fusion.4
  672.8 1.2 multiply_convert_fusion.1
  (94 shorter events, 4.9 us)
Async XLA Ops:
  7.2 382.1 %copy-start = (bf16[256,2048]{1,0:T(8,128)(2,1)S(1)}, bf16[256,2048]{1,0:T(8,128)(2,1)}, u32[]{:S(2)}) copy-start(bf16[256,2048]{1,0:T(8,128)(2,1)} %param.15) | copy-start | bytes 3145732
  7.2 137.7 %all-gather.4.cloned.1.call-start = ((), (), s32[]{:S(2)}) async-start(), calls=%async_computation | async-start | bytes 9437184 | tf_op jit(solution)/shard_map/all_gather | solution.py:15
  177.3 199.7 %copy-start.3 = (bf16[4,16,2048]{2,1,0:T(8,128)(2,1)S(1)}, bf16[4,16,2048]{2,1,0:T(8,128)(2,1)}, u32[]{:S(2)}) copy-start(bf16[4,16,2048]{2,1,0:T(8,128)(2,1)} %param.22) | copy-start | bytes 786436
  177.3 200.5 %copy-start.4 = (bf16[4,16,2048]{2,1,0:T(8,128)(2,1)S(1)}, bf16[4,16,2048]{2,1,0:T(8,128)(2,1)}, u32[]{:S(2)}) copy-start(bf16[4,16,2048]{2,1,0:T(8,128)(2,1)} %param.23) | copy-start | bytes 786436
  177.3 205.3 %copy-start.5 = (bf16[4,16,2048]{2,1,0:T(8,128)(2,1)S(1)}, bf16[4,16,2048]{2,1,0:T(8,128)(2,1)}, u32[]{:S(2)}) copy-start(bf16[4,16,2048]{2,1,0:T(8,128)(2,1)} %param.21) | copy-start | bytes 786436
  177.4 209.9 %copy-start.18 = (s32[16]{0:T(128)S(1)}, s32[16]{0:T(128)}, u32[]{:S(2)}) copy-start(s32[16]{0:T(128)} %param.25) | copy-start | bytes 196
  177.4 92.2 %collective-permute-start = (f32[4,16,128,128]{3,2,1,0:T(8,128)}, f32[4,16,128,128]{3,2,1,0:T(8,128)S(1)}, u32[]{:S(2)}, u32[]{:S(2)}) collective-permute-start(f32[4,16,128,128]{3,2,1,0:T(8,128)} %get-tuple-element.215), channel_id=1, source_target_pairs={{0,4},{4,0},{8,12},{12,8},{16,20},{20,16},{24,28},{28,24},{1,5},{5... | collective-permute-start | bytes 12582920 | tf_op jit(solution)/shard_map/ppermute | solution.py:132
  272.5 92.4 %collective-permute-start.1 = (f32[4,16,128,128]{3,2,1,0:T(8,128)S(1)}, f32[4,16,128,128]{3,2,1,0:T(8,128)S(1)}, u32[]{:S(2)}, u32[]{:S(2)}) collective-permute-start(f32[4,16,128,128]{3,2,1,0:T(8,128)S(1)} %add.130), channel_id=1, source_target_pairs={{0,8},{4,12},{8,0},{12,4},{16,24},{20,28},{24,16},{28,20},{1,9},{5... | collective-permute-start | bytes 12582920 | tf_op jit(solution)/shard_map/ppermute | solution.py:132
  367.6 189.2 %collective-permute-start.2 = (f32[4,16,128,128]{3,2,1,0:T(8,128)}, f32[4,16,128,128]{3,2,1,0:T(8,128)}, u32[]{:S(2)}, u32[]{:S(2)}) collective-permute-start(f32[4,16,128,128]{3,2,1,0:T(8,128)} %add.131), channel_id=1, source_target_pairs={{0,16},{4,20},{8,24},{12,28},{16,0},{20,4},{24,8},{28,12},{1,17},{... | collective-permute-start | bytes 12582920 | tf_op jit(solution)/shard_map/ppermute | solution.py:132
  563.3 10.2 %copy-start.8 = (bf16[16,16,128,1]{2,3,1,0:T(2,128)(2,1)S(1)}, bf16[16,16,128,1]{2,3,1,0:T(2,128)(2,1)}, u32[]{:S(2)}) copy-start(bf16[16,16,128,1]{2,3,1,0:T(2,128)(2,1)} %reshape.540) | copy-start | bytes 196612
  563.3 10.2 %copy-start.9 = (f32[2,8,16,128]{3,2,1,0:T(8,128)S(1)}, f32[2,8,16,128]{3,2,1,0:T(8,128)}, u32[]{:S(2)}) copy-start(f32[2,8,16,128]{3,2,1,0:T(8,128)} %copy.151) | copy-start | bytes 393220
  563.3 10.2 %copy-start.10 = (f32[2,8,16,128]{3,2,1,0:T(8,128)S(1)}, f32[2,8,16,128]{3,2,1,0:T(8,128)}, u32[]{:S(2)}) copy-start(f32[2,8,16,128]{3,2,1,0:T(8,128)} %copy.152) | copy-start | bytes 393220
  563.3 10.2 %copy-start.11 = (f32[2,8,16,128]{3,2,1,0:T(8,128)S(1)}, f32[2,8,16,128]{3,2,1,0:T(8,128)}, u32[]{:S(2)}) copy-start(f32[2,8,16,128]{3,2,1,0:T(8,128)} %copy.153) | copy-start | bytes 393220
  563.3 10.2 %copy-start.12 = (f32[2,8,16,128]{3,2,1,0:T(8,128)S(1)}, f32[2,8,16,128]{3,2,1,0:T(8,128)}, u32[]{:S(2)}) copy-start(f32[2,8,16,128]{3,2,1,0:T(8,128)} %copy.154) | copy-start | bytes 393220
  563.3 10.2 %copy-start.13 = (f32[2,8,16,128]{3,2,1,0:T(8,128)S(1)}, f32[2,8,16,128]{3,2,1,0:T(8,128)}, u32[]{:S(2)}) copy-start(f32[2,8,16,128]{3,2,1,0:T(8,128)} %copy.155) | copy-start | bytes 393220
  563.3 10.2 %copy-start.14 = (f32[2,8,16,128]{3,2,1,0:T(8,128)S(1)}, f32[2,8,16,128]{3,2,1,0:T(8,128)}, u32[]{:S(2)}) copy-start(f32[2,8,16,128]{3,2,1,0:T(8,128)} %copy.156) | copy-start | bytes 393220
  563.3 10.2 %copy-start.15 = (f32[2,8,16,128]{3,2,1,0:T(8,128)S(1)}, f32[2,8,16,128]{3,2,1,0:T(8,128)}, u32[]{:S(2)}) copy-start(f32[2,8,16,128]{3,2,1,0:T(8,128)} %copy.157) | copy-start | bytes 393220
  563.3 10.2 %copy-start.16 = (f32[2,8,16,128]{3,2,1,0:T(8,128)S(1)}, f32[2,8,16,128]{3,2,1,0:T(8,128)}, u32[]{:S(2)}) copy-start(f32[2,8,16,128]{3,2,1,0:T(8,128)} %copy.158) | copy-start | bytes 393220
  573.6 32.5 %copy-start.7 = (bf16[16,16,128,1]{2,3,1,0:T(2,128)(2,1)S(1)}, bf16[16,16,128,1]{2,3,1,0:T(2,128)(2,1)}, u32[]{:S(2)}) copy-start(bf16[16,16,128,1]{2,3,1,0:T(2,128)(2,1)} %reshape.538) | copy-start | bytes 196612
  606.1 23.1 %copy-start.6 = (bf16[16,16,128,1]{2,3,1,0:T(2,128)(2,1)S(1)}, bf16[16,16,128,1]{2,3,1,0:T(2,128)(2,1)}, u32[]{:S(2)}) copy-start(bf16[16,16,128,1]{2,3,1,0:T(2,128)(2,1)} %reshape.536) | copy-start | bytes 196612
  629.2 44.8 %copy-start.1 = (bf16[256,2048]{1,0:T(8,128)(2,1)S(1)}, bf16[256,2048]{1,0:T(8,128)(2,1)}, u32[]{:S(2)}) copy-start(bf16[256,2048]{1,0:T(8,128)(2,1)} %param.15) | copy-start | bytes 3145732
  647.3 23.7 %copy-start.17 = (f32[2048]{0:T(1024)S(1)}, f32[2048]{0:T(1024)}, u32[]{:S(2)}) copy-start(f32[2048]{0:T(1024)} %param.19) | copy-start | bytes 24580
  664.2 0.8 copy-start.2
Sparse Core Ops, SparseCore 0:
  17.6 127.2 all-gather.3
